TPU v7x, 32 devices: a whole 2x2x4 slice. The times are simulated.
32 devices in a mesh: bra: 8 (over z, x), ket: 2 (over y), mpo: 2 (over core).
Axes of the slice: x: 2, y: 2, z: 4, core: 2. Of those that a mesh axis runs over, the one named last changes fastest.
Arguments:
- left_env: bfloat16 [4, 3072, 3072], P('mpo', 'bra', 'ket'), may hold values from -6 to 6
- site_tensor: bfloat16 [3072, 4, 3072], P('bra', None, 'ket'), may hold values from -0.0546875 to 0.0546875
- block_values: float32 [12, 4, 4], replicated, may hold values from -3 to 3
- pair_in: int32 [12], replicated, may hold values from 0 to 3
- pair_out: int32 [12], replicated, may hold values from 0 to 3, as said below
Outputs:
- new_env: bfloat16 [4, 3072, 3072], P('mpo', 'bra', 'ket')
Inputs may be any that keep to these rules, and one draw needn't show every extreme that they name: `pair_out`: every component number 0 to 3 appears at least once.
All inputs are finite; a program needn't handle non-finite values.
Results may differ from a plain program's by a relative error of at most 0.018.
Values may be sent and summed in bfloat16 or wider, within the bound.
A program may use at most 192 MiB of HBM per device.

v0:
```python
import jax
import jax.numpy as jnp
from jax import lax
from jax.sharding import PartitionSpec as P

K = 4


def local(left_env, site_tensor, block_values, pair_in, pair_out):
    comps_loc = left_env.shape[0]
    rows_loc = left_env.shape[1]
    cols_loc = left_env.shape[2]
    phys = site_tensor.shape[1]
    comps = jnp.arange(K, dtype=jnp.int32)
    hot_out = (pair_out[:, None] == comps[None, :]).astype(jnp.float32)
    hot_in = (pair_in[:, None] == comps[None, :]).astype(jnp.float32)
    mixing = jnp.einsum(
        "pv,pw,pst->vswt", hot_out, hot_in, block_values, precision=lax.Precision.HIGHEST
    )
    splits = lax.axis_size("mpo")
    half_cols = cols_loc // splits
    own_start = lax.axis_index("mpo") * half_cols
    site_own = lax.dynamic_slice_in_dim(site_tensor, own_start, half_cols, 2)
    site_full = lax.all_gather(
        site_own.reshape(rows_loc, phys * half_cols), "bra", axis=0, tiled=True
    )
    piece = lax.all_gather(left_env, "ket", axis=2, tiled=True)
    piece = lax.all_gather(piece, "mpo", axis=0, tiled=True)
    comps_all, width = (piece.shape[0], piece.shape[2])
    half = jnp.dot(
        piece.reshape(comps_all * rows_loc, width), site_full, preferred_element_type=jnp.float32
    )
    half = half.astype(jnp.bfloat16).reshape(comps_all, rows_loc, phys, half_cols)
    mixed = jnp.einsum(
        "vswt,watc->savc", mixing, half.astype(jnp.float32), precision=lax.Precision.HIGHEST
    ).astype(jnp.bfloat16)
    mixed_pairs = mixed.reshape(phys * rows_loc, comps_all * half_cols)
    site_wide = lax.all_gather(jnp.transpose(site_tensor, (1, 0, 2)), "ket", axis=2, tiled=True)
    site_pairs = site_wide.reshape(phys * rows_loc, site_wide.shape[2])
    term = lax.dot_general(
        site_pairs, mixed_pairs, (((0,), (0,)), ((), ())), preferred_element_type=jnp.float32
    ).astype(jnp.bfloat16)
    owned = lax.psum_scatter(term, "bra", scatter_dimension=0, tiled=True)
    owned = jnp.transpose(owned.reshape(-1, comps_all, half_cols), (1, 0, 2))
    return lax.all_to_all(owned, "mpo", split_axis=0, concat_axis=2, tiled=True)


def solution(mesh):
    return jax.shard_map(
        local,
        mesh=mesh,
        in_specs=(P("mpo", "bra", "ket"), P("bra", None, "ket"), P(), P(), P()),
        out_specs=P("mpo", "bra", "ket"),
        check_vma=False,
    )
```

profile of v0, /device:TPU:0, one launch (start us, length us, event | category | flops | bytes accessed | tf_op | source)
XLA Modules:
  0.0 978.1 jit_solution(10487822228750793544)
XLA Ops:
  6.5 0.0 all-gather.7.cloned.1.call-start
  6.5 0.7 all-gather.7.cloned.1.call-update
  7.3 0.0 all-gather.9.cloned.1.call-start
  7.3 67.0 %all-gather.7.cloned.1.call-done = bf16[2,384,3072]{2,1,0:T(8,128)(2,1)} async-done(((bf16[2,384,1536]{2,1,0:T(8,128)(2,1)}), bf16[2,384,3072]{2,1,0:T(8,128)(2,1)}) %all-gather.7.cloned.1.call-update) | async-done | bytes 4718608 | tf_op jit(solution)/shard_map/all_gather | solution.py:27
  74.3 0.0 all-gather.9.cloned.1.call-update
  74.3 0.0 all-gather.5.cloned.1.call-start
  74.3 2.5 constant_dynamic-slice_fusion
  76.8 1.9 copy.27
  78.7 0.0 copy-start.1
  78.7 0.0 copy-start.2
  78.7 0.0 copy-start
  78.7 0.0 all-gather.5.cloned.1.call-update
  78.7 0.0 all-gather.11.cloned.1.call-start
  78.8 5.8 copy.34
  84.5 0.0 all-gather.11.cloned.1.call-update
  84.6 0.0 reduce-scatter.4.cloned.1.call-start
  84.6 0.0 copy-done.1
  84.6 0.0 copy-done.2
  84.7 0.0 copy-done
  84.7 0.3 convolution_bitcast_fusion
  85.0 12.5 %all-gather.9.cloned.1.call-done = bf16[4,384,3072]{2,1,0:T(8,128)(2,1)} async-done(((bf16[2,384,3072]{2,1,0:T(8,128)(2,1)}), bf16[4,384,3072]{2,1,0:T(8,128)(2,1)}) %all-gather.9.cloned.1.call-update) | async-done | bytes 9437200 | tf_op jit(solution)/shard_map/all_gather | solution.py:28
  97.5 365.1 %all-gather.5.cloned.1.call-done = bf16[3072,3072]{1,0:T(8,128)(2,1)} async-done(((bf16[384,3072]{1,0:T(8,128)(2,1)}), bf16[3072,3072]{1,0:T(8,128)(2,1)}) %all-gather.5.cloned.1.call-update) | async-done | bytes 18874384 | tf_op jit(solution)/shard_map/all_gather | solution.py:24
  462.6 36.7 %fusion = bf16[1536,3072]{0,1:T(8,128)(2,1)} fusion(bf16[3072,3072]{1,0:T(8,128)(2,1)} %all-gather.5.cloned.1.call-done, bf16[1536,3072]{1,0:T(8,128)(2,1)} %bitcast.57), kind=kOutput, calls=%fused_computation.3 | convolution fusion | flops 28995747840 | bytes 37748736 | tf_op jit(solution)/shard_map/dot_general | solution.py:30
  499.3 16.5 %reshape.22 = bf16[4,384,4,768]{1,0,3,2:T(4,128)(2,1)} reshape(bf16[1536,3072]{0,1:T(8,128)(2,1)} %fusion) | data formatting | bytes 18874368 | tf_op jit(solution)/shard_map/reshape | solution.py:33
  515.8 19.3 %copy.19 = bf16[4,384,4,768,1]{3,0,2,4,1:T(4,128)(2,1)} copy(bf16[4,384,4,768,1]{1,0,3,2,4:T(4,128)(2,1)} %bitcast.48) | data formatting | bytes 18874368 | tf_op jit(solution)/shard_map/reshape | solution.py:33
  535.0 20.1 %fusion.1 = bf16[4,384,4,768]{3,0,2,1:T(4,128)(2,1)S(1)} fusion(bf16[4,384,4,768,1]{3,0,2,4,1:T(4,128)(2,1)} %copy.19, f32[4,4,4,4,1]{1,2,3,0,4:T(4,128)S(1)} %convolution_bitcast_fusion), kind=kOutput, calls=%fused_computation.4 | convolution fusion | flops 910688256 | bytes 18875392 | tf_op jit(solution)/shard_map/vswt,watc->savc/dot_general | solution.py:34
  555.2 6.2 copy.15
  561.4 9.6 copy.28
  571.0 11.0 %all-gather.11.cloned.1.call-done = bf16[4,384,3072]{2,1,0:T(8,128)(2,1)} async-done(((bf16[4,384,1536]{2,1,0:T(8,128)(2,1)}), bf16[4,384,3072]{2,1,0:T(8,128)(2,1)}) %all-gather.11.cloned.1.call-update) | async-done | bytes 9437200 | tf_op jit(solution)/shard_map/all_gather | solution.py:38
  582.0 36.8 %convert_bitcast_fusion = bf16[3072,3072]{0,1:T(8,128)(2,1)} fusion(bf16[1536,3072]{1,0:T(8,128)(2,1)} %bitcast.51, bf16[1536,3072]{1,0:T(8,128)(2,1)} %bitcast.58), kind=kOutput, calls=%fused_computation.1 | convolution fusion | flops 29000466432 | bytes 37748736 | tf_op jit(solution)/shard_map/dot_general | solution.py:40
  618.8 24.6 %copy.25 = bf16[3072,3072]{1,0:T(8,128)(2,1)} copy(bf16[3072,3072]{0,1:T(8,128)(2,1)} %convert_bitcast_fusion) | data formatting | bytes 37748736
  643.4 0.0 reduce-scatter.4.cloned.1.call-update
  643.4 309.9 %reduce-scatter.4.cloned.1.call-done = bf16[384,3072]{1,0:T(8,128)(2,1)} async-done(((bf16[3072,3072]{1,0:T(8,128)(2,1)}), bf16[384,3072]{1,0:T(8,128)(2,1)}) %reduce-scatter.4.cloned.1.call-update) | async-done | bytes 2359312
  953.3 3.0 copy.26
  956.3 6.5 all_to_all.18
  962.9 6.0 copy.17
  968.8 2.8 all_to_all.16
  (1 shorter events, 0.0 us)
Async XLA Ops:
  6.5 67.7 %all-gather.7.cloned.1.call-start = ((), (), s32[]{:S(2)}) async-start(), calls=%async_computation.3 | async-start | bytes 7077888 | tf_op jit(solution)/shard_map/all_gather | solution.py:27
  7.3 90.2 %all-gather.9.cloned.1.call-start = ((), (), s32[]{:S(2)}) async-start(), calls=%async_computation.4 | async-start | bytes 14155776 | tf_op jit(solution)/shard_map/all_gather | solution.py:28
  74.3 388.3 %all-gather.5.cloned.1.call-start = ((), (), s32[]{:S(2)}) async-start(), calls=%async_computation.2 | async-start | bytes 21233664 | tf_op jit(solution)/shard_map/all_gather | solution.py:24
  78.7 5.9 copy-start.1
  78.7 5.9 copy-start.2
  78.7 5.9 copy-start
  78.7 503.3 %all-gather.11.cloned.1.call-start = ((), (), s32[]{:S(2)}) async-start(), calls=%async_computation.5 | async-start | bytes 14155776 | tf_op jit(solution)/shard_map/all_gather | solution.py:38
  84.6 868.7 %reduce-scatter.4.cloned.1.call-start = ((), (), s32[]{:S(2)}) async-start(), calls=%async_computation.6 | async-start | bytes 21233664
Sparse Core Ops, SparseCore 0:
  8.9 65.3 all-gather.6
  75.8 21.6 all-gather.8
  99.0 363.5 all-gather.4
  464.0 117.9 all-gather.10
  643.5 309.7 reduce-scatter.3
where the time goes:
time: 980 us; the launch traced here: 978 us
  waiting for transfers between devices  766 us (78%)
  local copies, waits for them, and re-layouts  98 us (10%)
  matrix products  93.9 us (10%)
  between operations  13.2 us (1%)
    all_gather x1, waiting for transfers between devices, local(): lax.all_gather(site_own.reshape(rows_loc, phys * half_cols), 'bra', axis=...  365 us
    unnamed x6, waiting for transfers between devices  311 us
    all_gather x1, waiting for transfers between devices, local(): piece = lax.all_gather(left_env, 'ket', axis=2, tiled=True)  67 us
    unnamed x11, local copies, waits for them, and re-layouts  44.8 us
    dot_general x1, matrix products, local(): lax.dot_general(site_pairs, mixed_pairs, (((0,), (0,)), ((), ())), prefer...  36.8 us
    dot_general x1, matrix products, local(): jnp.dot(piece.reshape(comps_all * rows_loc, width), site_full, preferred_...  36.7 us
    reshape x2, local copies, waits for them, and re-layouts, local(): half.astype(jnp.bfloat16).reshape(comps_all, rows_loc, phys, half_cols)  35.7 us
    dot_general x1, matrix products, local(): jnp.einsum('vswt,watc->savc', mixing, half.astype(jnp.float32), precision...  20.1 us
  transfers between devices with their start and end apart: 5, of which 5 were waited for; matrix products, arithmetic and copies ran while one was open for 12% of the time, Pallas kernels for 0%

commit v1 on v0

--- a/solution.py
+++ b/solution.py
@@ -1,9 +1,30 @@
+import functools
 import jax
 import jax.numpy as jnp
 from jax import lax
 from jax.sharding import PartitionSpec as P
 
 K = 4
+
+
+def supply_the_pipes(arr, dim_k):
+    v_next = list(arr.shape[1:])
+    v_next[dim_k] *= arr.shape[0]
+    return jnp.moveaxis(arr, 0, dim_k).reshape(v_next)
+
+
+def supply_all_members_all(block_here, shard_axis, array_axis):
+    k_all = lax.axis_size(shard_axis)
+    samples = [block_here]
+    log = [(ii, (ii + 1) % k_all) for ii in range(k_all)]
+    while len(samples) < k_all:
+        samples.append(lax.ppermute(samples[-1], axis_name=shard_axis, perm=log))
+    e_next = lax.axis_index(shard_axis)
+    samples = jnp.stack(samples)[(e_next - jnp.arange(k_all)) % k_all]
+    return supply_the_pipes(samples, array_axis)
+
+
+pipes_treat = functools.partial(supply_all_members_all, shard_axis="bra", array_axis=0)
 
 
 def local(left_env, site_tensor, block_values, pair_in, pair_out):
@@ -21,9 +42,7 @@
     half_cols = cols_loc // splits
     own_start = lax.axis_index("mpo") * half_cols
     site_own = lax.dynamic_slice_in_dim(site_tensor, own_start, half_cols, 2)
-    site_full = lax.all_gather(
-        site_own.reshape(rows_loc, phys * half_cols), "bra", axis=0, tiled=True
-    )
+    site_full = pipes_treat(site_own.reshape(rows_loc, phys * half_cols))
     piece = lax.all_gather(left_env, "ket", axis=2, tiled=True)
     piece = lax.all_gather(piece, "mpo", axis=0, tiled=True)
     comps_all, width = (piece.shape[0], piece.shape[2])

time: 980 us -> 943 us (0.962)
  waiting for transfers between devices: 766 us -> 670 us
  local copies, waits for them, and re-layouts: 98 us -> 136 us
  other arithmetic: 0.01 us -> 16.2 us
    all_gather x1 -> x0, waiting for transfers between devices: 365 us -> none  [local(): lax.all_gather(site_own.reshape(rows_loc, phys * half_cols), 'bra', axis=...]
    ppermute x0 -> x7, waiting for transfers between devices: none -> 303 us  [supply_all_members_all(): samples.append(lax.ppermute(samples[-1], axis_name=shard_axis, perm=log))]
    gather x0 -> x3, local copies, waits for them, and re-layouts: none -> 24.4 us  [supply_all_members_all(): samples = jnp.stack(samples)[(e_next - jnp.arange(k_all)) % k_all]]
    unnamed x0 -> x1, other arithmetic: none -> 16.1 us
    all_gather x1, waiting for transfers between devices: 12.5 us -> 0.01 us  [local(): piece = lax.all_gather(piece, 'mpo', axis=0, tiled=True)]
    all_gather x1, waiting for transfers between devices: 11 us -> 0.01 us  [local(): lax.all_gather(jnp.transpose(site_tensor, (1, 0, 2)), 'ket', axis=2, tile...]
    unnamed x11 -> x26, local copies, waits for them, and re-layouts: 44.8 us -> 55.3 us
    unnamed x6 -> x5, waiting for transfers between devices: 311 us -> 308 us
  transfers between devices with their start and end apart: 5 -> 11, of which waited for: 5 -> 8; matrix products, arithmetic and copies ran while one was open for 12% -> 18% of each run, Pallas kernels for 0% -> 0%
where the time goes in v1:
time: 943 us; the launch traced here: 941 us
  waiting for transfers between devices  670 us (71%)
  local copies, waits for them, and re-layouts  136 us (14%)
  matrix products  93.9 us (10%)
  other arithmetic  16.2 us (2%)
  between operations  13.3 us (1%)
    unnamed x5, waiting for transfers between devices  308 us
    ppermute x7, waiting for transfers between devices, supply_all_members_all(): samples.append(lax.ppermute(samples[-1], axis_name=shard_axis, perm=log))  303 us
    all_gather x1, waiting for transfers between devices, local(): piece = lax.all_gather(left_env, 'ket', axis=2, tiled=True)  59.6 us
    unnamed x26, local copies, waits for them, and re-layouts  55.3 us
    dot_general x1, matrix products, local(): lax.dot_general(site_pairs, mixed_pairs, (((0,), (0,)), ((), ())), prefer...  36.8 us
    dot_general x1, matrix products, local(): jnp.dot(piece.reshape(comps_all * rows_loc, width), site_full, preferred_...  36.7 us
    reshape x2, local copies, waits for them, and re-layouts, local(): half.astype(jnp.bfloat16).reshape(comps_all, rows_loc, phys, half_cols)  35.7 us
    gather x3, local copies, waits for them, and re-layouts, supply_all_members_all(): samples = jnp.stack(samples)[(e_next - jnp.arange(k_all)) % k_all]  24.4 us
  transfers between devices with their start and end apart: 11, of which 8 were waited for; matrix products, arithmetic and copies ran while one was open for 18% of the time, Pallas kernels for 0%

profile of v1, /device:TPU:0, one launch (start us, length us, event | category | flops | bytes accessed | tf_op | source)
XLA Modules:
  0.0 940.8 jit_solution(12870490741794794804)
XLA Ops:
  6.5 0.7 all-gather.4.cloned.1.call-update
  7.3 0.0 all-gather.6.cloned.1.call-start
  7.3 2.5 constant_dynamic-slice_fusion
  9.8 1.9 copy.27
  11.7 3.0 collective-permute-start
  14.6 59.6 %all-gather.4.cloned.1.call-done = bf16[2,384,3072]{2,1,0:T(8,128)(2,1)} async-done(((bf16[2,384,1536]{2,1,0:T(8,128)(2,1)}), bf16[2,384,3072]{2,1,0:T(8,128)(2,1)}) %all-gather.4.cloned.1.call-update) | async-done | bytes 4718608 | tf_op jit(solution)/shard_map/all_gather | solution.py:46
  74.3 0.0 all-gather.6.cloned.1.call-update
  74.3 0.0 all-gather.8.cloned.1.call-start
  74.4 1.5 collective-permute-start.1
  75.9 54.3 %collective-permute-done.1 = bf16[384,3072]{1,0:T(8,128)(2,1)S(1)} collective-permute-done((bf16[384,3072]{1,0:T(8,128)(2,1)}, bf16[384,3072]{1,0:T(8,128)(2,1)S(1)}, u32[]{:S(2)}, u32[]{:S(2)}) %collective-permute-start.1) | collective-permute-done | bytes 2359328 | tf_op jit(solution)/shard_map/ppermute | solution.py:21
  130.2 1.4 copy-done
  131.6 54.7 %collective-permute-done.2 = bf16[384,3072]{1,0:T(8,128)(2,1)S(1)} collective-permute-done((bf16[384,3072]{1,0:T(8,128)(2,1)S(1)}, bf16[384,3072]{1,0:T(8,128)(2,1)S(1)}, u32[]{:S(2)}, u32[]{:S(2)}) %collective-permute-start.2) | collective-permute-done | bytes 2359328 | tf_op jit(solution)/shard_map/ppermute | solution.py:21
  186.3 1.4 copy-done.2
  187.7 53.9 %collective-permute-done.3 = bf16[384,3072]{1,0:T(8,128)(2,1)} collective-permute-done((bf16[384,3072]{1,0:T(8,128)(2,1)S(1)}, bf16[384,3072]{1,0:T(8,128)(2,1)}, u32[]{:S(2)}, u32[]{:S(2)}) %collective-permute-start.3) | collective-permute-done | bytes 2359328 | tf_op jit(solution)/shard_map/ppermute | solution.py:21
  241.6 5.4 copy.34
  247.0 0.0 all-gather.8.cloned.1.call-update
  247.0 0.0 reduce-scatter.4.cloned.1.call-start
  247.1 2.9 stack_reshape.3
  250.1 0.3 convolution_bitcast_fusion
  250.4 2.0 constant_dynamic-update-slice_fusion
  252.4 42.4 %collective-permute-done.4 = bf16[384,3072]{1,0:T(8,128)(2,1)} collective-permute-done((bf16[384,3072]{1,0:T(8,128)(2,1)}, bf16[384,3072]{1,0:T(8,128)(2,1)}, u32[]{:S(2)}, u32[]{:S(2)}) %collective-permute-start.4) | collective-permute-done | bytes 2359328 | tf_op jit(solution)/shard_map/ppermute | solution.py:21
  294.9 1.8 bitcast_dynamic-update-slice_fusion.6
  296.7 0.2 bitcast_dynamic-update-slice_fusion.5
  296.9 0.2 bitcast_dynamic-update-slice_fusion.4
  297.1 50.1 %collective-permute-done.5 = bf16[384,3072]{1,0:T(8,128)(2,1)S(1)} collective-permute-done((bf16[384,3072]{1,0:T(8,128)(2,1)}, bf16[384,3072]{1,0:T(8,128)(2,1)S(1)}, u32[]{:S(2)}, u32[]{:S(2)}) %collective-permute-start.5) | collective-permute-done | bytes 2359328 | tf_op jit(solution)/shard_map/ppermute | solution.py:21
  347.2 1.8 bitcast_dynamic-update-slice_fusion.3
  349.0 1.8 bitcast_dynamic-update-slice_fusion.2
  350.8 0.2 bitcast_dynamic-update-slice_fusion.1
  351.0 47.4 %collective-permute-done.6 = bf16[384,3072]{1,0:T(8,128)(2,1)S(1)} collective-permute-done((bf16[384,3072]{1,0:T(8,128)(2,1)S(1)}, bf16[384,3072]{1,0:T(8,128)(2,1)S(1)}, u32[]{:S(2)}, u32[]{:S(2)}) %collective-permute-start.6) | collective-permute-done | bytes 2359328 | tf_op jit(solution)/shard_map/ppermute | solution.py:21
  398.4 0.2 bitcast_dynamic-update-slice_fusion
  398.6 6.8 fusion.12
  405.4 8.9 gather_fusion
  414.2 8.8 gather_fusion.1
  423.0 16.1 %pad_maximum_fusion = bf16[8,384,3072]{2,1,0:T(8,128)(2,1)} fusion(bf16[8,384,1536]{2,1,0:T(8,128)(2,1)} %gather_fusion.1, bf16[8,384,1536]{2,1,0:T(8,128)(2,1)} %gather_fusion), kind=kLoop, calls=%fused_computation.2 | loop fusion | flops 37748736 | bytes 37748736
  439.2 36.7 %fusion = bf16[1536,3072]{0,1:T(8,128)(2,1)} fusion(bf16[3072,3072]{1,0:T(8,128)(2,1)} %bitcast.68, bf16[1536,3072]{1,0:T(8,128)(2,1)} %bitcast.74), kind=kOutput, calls=%fused_computation.6 | convolution fusion | flops 28995747840 | bytes 37748736 | tf_op jit(solution)/shard_map/dot_general | solution.py:49
  475.9 16.4 %reshape.75 = bf16[4,384,4,768]{1,0,3,2:T(4,128)(2,1)} reshape(bf16[1536,3072]{0,1:T(8,128)(2,1)} %fusion) | data formatting | bytes 18874368 | tf_op jit(solution)/shard_map/reshape | solution.py:52
  492.3 19.2 %copy.19 = bf16[4,384,4,768,1]{3,0,2,4,1:T(4,128)(2,1)} copy(bf16[4,384,4,768,1]{1,0,3,2,4:T(4,128)(2,1)} %bitcast.65) | data formatting | bytes 18874368 | tf_op jit(solution)/shard_map/reshape | solution.py:52
  511.5 20.1 %fusion.1 = bf16[4,384,4,768]{3,0,2,1:T(4,128)(2,1)S(1)} fusion(bf16[4,384,4,768,1]{3,0,2,4,1:T(4,128)(2,1)} %copy.19, f32[4,4,4,4,1]{1,2,3,0,4:T(4,128)S(1)} %convolution_bitcast_fusion), kind=kOutput, calls=%fused_computation.7 | convolution fusion | flops 910688256 | bytes 18875392 | tf_op jit(solution)/shard_map/vswt,watc->savc/dot_general | solution.py:53
  531.7 6.2 copy.15
  537.9 9.6 %copy.28 = bf16[192,8,4,768]{3,1,2,0:T(8,128)(2,1)} copy(bf16[192,8,4,768]{3,2,1,0:T(4,128)(2,1)} %bitcast.66) | data formatting | bytes 18874368
  547.5 36.8 %convert_bitcast_fusion = bf16[3072,3072]{0,1:T(8,128)(2,1)} fusion(bf16[1536,3072]{1,0:T(8,128)(2,1)} %bitcast.70, bf16[1536,3072]{1,0:T(8,128)(2,1)} %bitcast.75), kind=kOutput, calls=%fused_computation.4 | convolution fusion | flops 29000466432 | bytes 37748736 | tf_op jit(solution)/shard_map/dot_general | solution.py:59
  584.3 24.7 %copy.25 = bf16[3072,3072]{1,0:T(8,128)(2,1)} copy(bf16[3072,3072]{0,1:T(8,128)(2,1)} %convert_bitcast_fusion) | data formatting | bytes 37748736
  608.9 0.0 reduce-scatter.4.cloned.1.call-update
  608.9 307.0 %reduce-scatter.4.cloned.1.call-done = bf16[384,3072]{1,0:T(8,128)(2,1)} async-done(((bf16[3072,3072]{1,0:T(8,128)(2,1)}), bf16[384,3072]{1,0:T(8,128)(2,1)}) %reduce-scatter.4.cloned.1.call-update) | async-done | bytes 2359312
  916.0 3.0 copy.26
  919.0 6.6 all_to_all.18
  925.5 6.0 copy.17
  931.5 2.8 all_to_all.16
  (24 shorter events, 0.1 us)
Async XLA Ops:
  6.5 67.7 %all-gather.4.cloned.1.call-start = ((), (), s32[]{:S(2)}) async-start(), calls=%async_computation.2 | async-start | bytes 7077888 | tf_op jit(solution)/shard_map/all_gather | solution.py:46
  7.3 431.9 %all-gather.6.cloned.1.call-start = ((), (), s32[]{:S(2)}) async-start(), calls=%async_computation.3 | async-start | bytes 14155776 | tf_op jit(solution)/shard_map/all_gather | solution.py:47
  11.7 62.7 %collective-permute-start = (bf16[384,3072]{1,0:T(8,128)(2,1)}, bf16[384,3072]{1,0:T(8,128)(2,1)}, u32[]{:S(2)}, u32[]{:S(2)}) collective-permute-start(bf16[384,3072]{1,0:T(8,128)(2,1)} %bitcast.32), channel_id=1, source_target_pairs={{0,4},{4,8},{8,12},{12,16},{16,20},{20,24},{24,28},{28,0},{1,5},{5... | collective-permute-start | bytes 7077896 | tf_op jit(solution)/shard_map/ppermute | solution.py:21
  74.3 175.7 %copy-start.5 = (s32[12]{0:T(128)S(1)}, s32[12]{0:T(128)}, u32[]{:S(2)}) copy-start(s32[12]{0:T(128)} %param.8) | copy-start | bytes 148
  74.3 175.7 %copy-start.6 = (s32[12]{0:T(128)S(1)}, s32[12]{0:T(128)}, u32[]{:S(2)}) copy-start(s32[12]{0:T(128)} %param.9) | copy-start | bytes 148
  74.3 175.8 %copy-start.4 = (f32[12,4,4]{0,2,1:T(4,128)S(1)}, f32[12,4,4]{0,2,1:T(4,128)}, u32[]{:S(2)}) copy-start(f32[12,4,4]{0,2,1:T(4,128)} %param.7) | copy-start | bytes 2308
  74.3 473.2 %all-gather.8.cloned.1.call-start = ((), (), s32[]{:S(2)}) async-start(), calls=%async_computation.4 | async-start | bytes 14155776 | tf_op jit(solution)/shard_map/all_gather | solution.py:57
  74.4 55.8 %collective-permute-start.1 = (bf16[384,3072]{1,0:T(8,128)(2,1)}, bf16[384,3072]{1,0:T(8,128)(2,1)S(1)}, u32[]{:S(2)}, u32[]{:S(2)}) collective-permute-start(bf16[384,3072]{1,0:T(8,128)(2,1)} %collective-permute-done), channel_id=1, source_target_pairs={{0,4},{4,8},{8,12},{12,16},{16,20},{20,24},{24,28},{28,0},{1,5},{5... | collective-permute-start | bytes 7077896 | tf_op jit(solution)/shard_map/ppermute | solution.py:21
  130.2 1.4 copy-start
  131.6 54.7 %collective-permute-start.2 = (bf16[384,3072]{1,0:T(8,128)(2,1)S(1)}, bf16[384,3072]{1,0:T(8,128)(2,1)S(1)}, u32[]{:S(2)}, u32[]{:S(2)}) collective-permute-start(bf16[384,3072]{1,0:T(8,128)(2,1)S(1)} %collective-permute-done.1), channel_id=1, source_target_pairs={{0,4},{4,8},{8,12},{12,16},{16,20},{20,24},{24,28},{28,0},{1,5},{5... | collective-permute-start | bytes 7077896 | tf_op jit(solution)/shard_map/ppermute | solution.py:21
  186.3 1.4 copy-start.2
  187.7 53.9 %collective-permute-start.3 = (bf16[384,3072]{1,0:T(8,128)(2,1)S(1)}, bf16[384,3072]{1,0:T(8,128)(2,1)}, u32[]{:S(2)}, u32[]{:S(2)}) collective-permute-start(bf16[384,3072]{1,0:T(8,128)(2,1)S(1)} %collective-permute-done.2), channel_id=1, source_target_pairs={{0,4},{4,8},{8,12},{12,16},{16,20},{20,24},{24,28},{28,0},{1,5},{5... | collective-permute-start | bytes 7077896 | tf_op jit(solution)/shard_map/ppermute | solution.py:21
  241.6 53.3 %collective-permute-start.4 = (bf16[384,3072]{1,0:T(8,128)(2,1)}, bf16[384,3072]{1,0:T(8,128)(2,1)}, u32[]{:S(2)}, u32[]{:S(2)}) collective-permute-start(bf16[384,3072]{1,0:T(8,128)(2,1)} %collective-permute-done.3), channel_id=1, source_target_pairs={{0,4},{4,8},{8,12},{12,16},{16,20},{20,24},{24,28},{28,0},{1,5},{5... | collective-permute-start | bytes 7077896 | tf_op jit(solution)/shard_map/ppermute | solution.py:21
  247.0 669.0 %reduce-scatter.4.cloned.1.call-start = ((), (), s32[]{:S(2)}) async-start(), calls=%async_computation.5 | async-start | bytes 21233664
  250.0 46.7 %copy-start.1 = (bf16[384,3072]{1,0:T(8,128)(2,1)S(1)}, bf16[384,3072]{1,0:T(8,128)(2,1)}, u32[]{:S(2)}) copy-start(bf16[384,3072]{1,0:T(8,128)(2,1)} %copy-done) | copy-start | bytes 7077892
  250.0 46.9 %copy-start.3 = (bf16[384,3072]{1,0:T(8,128)(2,1)S(1)}, bf16[384,3072]{1,0:T(8,128)(2,1)}, u32[]{:S(2)}) copy-start(bf16[384,3072]{1,0:T(8,128)(2,1)} %copy-done.2) | copy-start | bytes 7077892
  294.9 52.3 %collective-permute-start.5 = (bf16[384,3072]{1,0:T(8,128)(2,1)}, bf16[384,3072]{1,0:T(8,128)(2,1)S(1)}, u32[]{:S(2)}, u32[]{:S(2)}) collective-permute-start(bf16[384,3072]{1,0:T(8,128)(2,1)} %collective-permute-done.4), channel_id=1, source_target_pairs={{0,4},{4,8},{8,12},{12,16},{16,20},{20,24},{24,28},{28,0},{1,5},{5... | collective-permute-start | bytes 7077896 | tf_op jit(solution)/shard_map/ppermute | solution.py:21
  347.2 51.2 %collective-permute-start.6 = (bf16[384,3072]{1,0:T(8,128)(2,1)S(1)}, bf16[384,3072]{1,0:T(8,128)(2,1)S(1)}, u32[]{:S(2)}, u32[]{:S(2)}) collective-permute-start(bf16[384,3072]{1,0:T(8,128)(2,1)S(1)} %collective-permute-done.5), channel_id=1, source_target_pairs={{0,4},{4,8},{8,12},{12,16},{16,20},{20,24},{24,28},{28,0},{1,5},{5... | collective-permute-start | bytes 7077896 | tf_op jit(solution)/shard_map/ppermute | solution.py:21
Sparse Core Ops, SparseCore 0:
  8.9 65.3 all-gather.3
  75.8 21.6 all-gather.5
  247.1 118.7 all-gather.7
  609.1 306.8 reduce-scatter.3
